TPU v7x, 32 devices: a whole 2x2x4 slice. The times are simulated.
32 devices in a mesh: pipe: 4 (over y, x), dp: 2 (over core), expert: 4 (over z).
Axes of the slice: x: 2, y: 2, z: 4, core: 2. Of those that a mesh axis runs over, the one named last changes fastest.
Arguments:
- embedded: bfloat16 [1024, 2048], P(('dp', 'expert')), may hold values from -6 to 6
- section_out: bfloat16 [4, 1024, 2048], P('pipe', ('dp', 'expert')), may hold values from -6 to 6
- expert_ids: int32 [4, 1024, 6], P('pipe', ('dp', 'expert')), may hold values from 0 to 31, all different within a row
- route_weights: float32 [4, 1024, 6], P('pipe', ('dp', 'expert')), may hold values from 0.02 to 0.6
- valid_tokens: int32 [4, 8], P('pipe', ('dp', 'expert')), may hold values from 32 to 96, as said below
- w_gate_up: bfloat16 [4, 64, 2048, 704], P('pipe', 'expert'), may hold values from -0.125 to 0.125
- w_down: bfloat16 [4, 64, 352, 2048], P('pipe', 'expert'), may hold values from -0.21875 to 0.21875
Outputs:
- mixed: bfloat16 [4, 1024, 2048], P('pipe', ('dp', 'expert'))
- balance: float32 [4], P('pipe')
Inputs may be any that keep to these rules, and one draw needn't show every extreme that they name: `expert_ids`: each row names 6 different experts. The first valid_tokens[s, g] rows of group g are real, the rest padding.
All inputs are finite; a program needn't handle non-finite values.
Results may differ from a plain program's by a relative error of at most 0.0027.
Values may be sent and summed in bfloat16 or wider, within the bound.
A program may use at most 128 MiB of HBM per device.

v0:
```python
import jax
import jax.numpy as jnp
from jax import lax
from jax.sharding import PartitionSpec as P

EXPERTS = 32
TOP = 6
CAP = 8


def shifted(block, axis, distance):
    devices = range(lax.axis_size(axis))
    route = [(i - distance, i) for i in devices if i - distance in devices]
    return lax.ppermute(block, axis, route)


def route(expert_ids, route_weights, live_count):
    tok_count = expert_ids.shape[0]
    live_mask = (jnp.arange(tok_count, dtype=jnp.int32) < live_count)[:, None, None]
    chosen = (
        (expert_ids[:, :, None] == jnp.arange(EXPERTS, dtype=jnp.int32)[None, None, :]) & live_mask
    ).astype(jnp.int32)
    flat_picks = chosen.reshape(tok_count * TOP, EXPERTS)
    earlier = jnp.cumsum(flat_picks, axis=0) - flat_picks
    slot_rank = jnp.sum(earlier * flat_picks, axis=1).reshape(tok_count, TOP)
    kept_mask = (jnp.sum(chosen, axis=2) > 0) & (slot_rank < CAP)
    slots = jnp.where(kept_mask, expert_ids * CAP + slot_rank, -1)
    counts = jnp.sum(flat_picks, axis=0).astype(jnp.float32)
    prob_sums = jnp.sum(chosen.astype(jnp.float32) * route_weights[:, :, None], axis=(0, 1))
    columns = jnp.arange(EXPERTS * CAP, dtype=jnp.int32)
    slot_hits = slots[:, :, None] == columns[None, None, :]
    dispatch = jnp.sum(slot_hits, axis=1).astype(jnp.float32)
    mixing = jnp.sum(jnp.where(slot_hits, route_weights[:, :, None], jnp.float32(0.0)), axis=1)
    return (dispatch, mixing, counts, prob_sums)


def expert_ffn(tokens, w_in, w_out):
    gate_up = jnp.einsum("skcd,kdf->skcf", tokens, w_in, preferred_element_type=jnp.float32)
    hidden_width = w_out.shape[1]
    hidden = (jax.nn.silu(gate_up[..., :hidden_width]) * gate_up[..., hidden_width:]).astype(
        jnp.bfloat16
    )
    return jnp.einsum("skcf,kfd->skcd", hidden, w_out, preferred_element_type=jnp.float32).astype(
        jnp.bfloat16
    )


def on_device(embedded, section_out, expert_ids, route_weights, valid_tokens, w_gate_up, w_down):
    arrived = shifted(section_out[0], "pipe", 1)
    incoming = jnp.where(lax.axis_index("pipe") == 0, embedded, arrived)
    dispatch, mixing, counts, prob_sums = route(expert_ids[0], route_weights[0], valid_tokens[0, 0])
    live_total = valid_tokens[0, 0].astype(jnp.float32)
    totals = lax.psum((counts, prob_sums, live_total), ("dp", "expert"))
    gathered = jnp.einsum(
        "ts,td->sd", dispatch.astype(jnp.bfloat16), incoming, preferred_element_type=jnp.float32
    ).astype(jnp.bfloat16)
    devices = lax.axis_size("expert")
    couples = devices // 2
    local_count = w_gate_up.shape[1]
    model_width = incoming.shape[1]
    grouped = gathered.reshape(couples, local_count, CAP, model_width)
    weights_in = w_gate_up[0]
    weights_out = w_down[0]
    sent = jnp.broadcast_to(grouped[:, None], (couples, 2, local_count, CAP, model_width))
    sent = sent.reshape(devices, local_count * CAP, model_width)
    arrived_rows = lax.all_to_all(sent, "expert", split_axis=0, concat_axis=0, tiled=True).reshape(
        devices, local_count, CAP, model_width
    )
    partial_value = expert_ffn(arrived_rows, weights_in, weights_out)
    returned = lax.all_to_all(
        partial_value.reshape(devices, local_count * CAP, model_width),
        "expert",
        split_axis=0,
        concat_axis=0,
        tiled=True,
    )
    returned = returned.reshape(couples, 2, local_count, CAP, model_width)
    merged = (returned[:, 0].astype(jnp.float32) + returned[:, 1].astype(jnp.float32)).astype(
        jnp.bfloat16
    )
    merged = merged.reshape(EXPERTS * CAP, model_width)
    branch = jnp.dot(mixing, merged.astype(jnp.float32), precision=lax.Precision.HIGHEST)
    result = (incoming.astype(jnp.float32) + branch).astype(jnp.bfloat16)
    total_counts, total_probs, total_live = totals
    balance = EXPERTS * jnp.sum(total_counts * total_probs) / (TOP * total_live * total_live)
    return (result[None], balance.reshape(1))


def solution(mesh):
    return jax.shard_map(
        on_device,
        mesh=mesh,
        in_specs=(
            P(("dp", "expert"), None),
            P("pipe", ("dp", "expert"), None),
            P("pipe", ("dp", "expert"), None),
            P("pipe", ("dp", "expert"), None),
            P("pipe", ("dp", "expert")),
            P("pipe", "expert", None, None),
            P("pipe", "expert", None, None),
        ),
        out_specs=(P("pipe", ("dp", "expert"), None), P("pipe")),
        check_vma=False,
    )
```

profile of v0, /device:TPU:0, one launch (start us, length us, event | category | flops | bytes accessed | tf_op | source)
XLA Modules:
  0.0 168.3 jit_solution(4044405793539294508)
XLA Ops:
  0.6 4.9 %collective-permute-start = (bf16[128,2048]{1,0:T(8,128)(2,1)}, bf16[128,2048]{1,0:T(8,128)(2,1)S(1)}, u32[]{:S(2)}, u32[]{:S(2)}) collective-permute-start(bf16[128,2048]{1,0:T(8,128)(2,1)} %bitcast.72), channel_id=1, source_target_pairs={{0,8},{8,16},{16,24},{1,9},{9,17},{17,25},{2,10},{10,18},{18,26},{... | collective-permute-start | bytes 1572872 | tf_op jit(solution)/shard_map/ppermute | solution.py:14
  6.2 0.1 and.35
  6.3 0.2 and.39
  6.4 0.1 and.36
  6.6 0.8 copy.21
  7.4 0.1 eq.59
  7.5 0.1 eq.55
  7.7 0.7 copy.45
  8.4 1.7 %reduce-window.6 = s32[32,6,128]{2,0,1:T(8,128)S(1)} reduce-window(s32[32,6,128]{2,0,1:T(8,128)S(1)} %fusion.27, s32[]{:T(128)} %constant.9.clone.1), window={size=1x1x128 pad=0_0x0_0x127_0}, to_apply=%region_1.2 | reduce-window | flops 3121152 | bytes 196612 | tf_op jit(solution)/shard_map/reduce-window
  10.1 0.3 slice_reduce_fusion
  10.4 0.2 convert_reduce_fusion.1
  10.6 0.1 reshape.79
  10.7 0.1 copy.24
  10.8 0.7 add_select_fusion
  11.5 0.2 convert_reduce_fusion
  11.7 5.3 %collective-permute-done = bf16[128,2048]{1,0:T(8,128)(2,1)S(1)} collective-permute-done((bf16[128,2048]{1,0:T(8,128)(2,1)}, bf16[128,2048]{1,0:T(8,128)(2,1)S(1)}, u32[]{:S(2)}, u32[]{:S(2)}) %collective-permute-start) | collective-permute-done | bytes 524320 | tf_op jit(solution)/shard_map/ppermute | solution.py:14
  17.0 1.5 convolution_convert_fusion
  18.5 0.3 broadcast_in_dim.37
  18.8 52.0 %all_to_all.10 = bf16[4,128,2048]{2,1,0:T(8,128)(2,1)S(1)} all-to-all(bf16[4,128,2048]{2,1,0:T(8,128)(2,1)S(1)} %bitcast.64), channel_id=1, replica_groups=mesh['pipe'=4,'dp'=2,'expert'=4] {'expert'}, dimensions={0} | all-to-all | bytes 4194304 | tf_op jit(solution)/shard_map/all_to_all | solution.py:66
  70.8 18.7 %fusion.11 = f32[4,16,8,704]{3,2,0,1:T(8,128)S(1)} fusion(bf16[1,16,2048,704]{2,3,1,0:T(8,128)(2,1)} %param.12, bf16[4,128,2048]{2,1,0:T(8,128)(2,1)S(1)} %all_to_all.10), kind=kOutput, calls=%fused_computation.10 | convolution fusion | flops 1476395008 | bytes 49676288 | tf_op jit(solution)/shard_map/skcd,kdf->skcf/dot_general | solution.py:38
  89.4 11.4 %fusion.7 = bf16[4,16,8,2048]{3,2,0,1:T(8,128)(2,1)S(1)} fusion(bf16[1,16,352,2048]{3,2,1,0:T(8,128)(2,1)} %param.13, f32[4,16,8,704]{3,2,0,1:T(8,128)S(1)} %fusion.11), kind=kOutput, calls=%fused_computation.5 | convolution fusion | flops 740327424 | bytes 26607616 | tf_op jit(solution)/shard_map/skcf,kfd->skcd/dot_general | solution.py:43
  100.8 1.5 copy.43
  102.3 0.0 copy-start.1
  102.3 3.7 %all-to-all-start.1 = ((bf16[4,128,2048]{2,1,0:T(8,128)(2,1)}), bf16[4,128,2048]{2,1,0:T(8,128)(2,1)S(1)}, u32[]{:S(2)}, u32[]{:S(2)}) async-start(bf16[4,128,2048]{2,1,0:T(8,128)(2,1)} %bitcast.63), calls=%async_computation.1 | async-start | bytes 4194304 | tf_op jit(solution)/shard_map/all_to_all | solution.py:70
  106.1 0.0 copy-start
  106.1 0.0 copy-done.1
  106.1 0.1 fusion.23
  106.3 56.2 %all-reduce = (f32[32]{0:T(128)S(1)}, f32[32]{0:T(128)S(1)}, f32[]{:T(128)}) all-reduce(f32[32]{0:T(128)S(1)} %convert_element_type.80, f32[32]{0:T(128)S(1)} %fusion.23, f32[]{:T(128)S(6)} %convert_element_type.82), channel_id=1, replica_groups=mesh['pipe'=4,'dp'=2,'expert'=4] {'dp','expert'}, use_global_device_ids=true, to_apply=%region_7.8 | all-reduce | flops 65 | bytes 520 | tf_op jit(solution)/shard_map/psum | solution.py:53
  163.7 0.6 multiply_reduce_fusion
  165.0 0.3 select_reduce_fusion
  165.3 0.0 all-to-all-done.1
  165.3 0.4 add_convert_fusion
  165.7 0.0 copy-done
  165.7 1.4 fusion.17
  (6 shorter events, 0.1 us)
Async XLA Ops:
  0.6 16.4 %collective-permute-start = (bf16[128,2048]{1,0:T(8,128)(2,1)}, bf16[128,2048]{1,0:T(8,128)(2,1)S(1)}, u32[]{:S(2)}, u32[]{:S(2)}) collective-permute-start(bf16[128,2048]{1,0:T(8,128)(2,1)} %bitcast.72), channel_id=1, source_target_pairs={{0,8},{8,16},{16,24},{1,9},{9,17},{17,25},{2,10},{10,18},{18,26},{... | collective-permute-start | bytes 1572872 | tf_op jit(solution)/shard_map/ppermute | solution.py:14
  102.3 3.8 %copy-start.1 = (f32[1,128,6]{1,0,2:T(1,128)S(1)}, f32[1,128,6]{1,0,2:T(1,128)}, u32[]{:S(2)}) copy-start(f32[1,128,6]{1,0,2:T(1,128)} %param.10) | copy-start | bytes 9220
  102.3 63.0 %all-to-all-start.1 = ((bf16[4,128,2048]{2,1,0:T(8,128)(2,1)}), bf16[4,128,2048]{2,1,0:T(8,128)(2,1)S(1)}, u32[]{:S(2)}, u32[]{:S(2)}) async-start(bf16[4,128,2048]{2,1,0:T(8,128)(2,1)} %bitcast.63), calls=%async_computation.1 | async-start | bytes 4194304 | tf_op jit(solution)/shard_map/all_to_all | solution.py:70
  106.1 59.6 %copy-start = (bf16[128,2048]{1,0:T(8,128)(2,1)S(1)}, bf16[128,2048]{1,0:T(8,128)(2,1)}, u32[]{:S(2)}) copy-start(bf16[128,2048]{1,0:T(8,128)(2,1)} %param.7) | copy-start | bytes 1572868
where the time goes:
time: 169 us; the launch traced here: 168 us
  blocking collectives  108 us (64%)
  matrix products  33 us (20%)
  starting transfers between devices  8.64 us (5%)
  waiting for transfers between devices  5.32 us (3%)
  between operations  4.57 us (3%)
  local copies, waits for them, and re-layouts  4.34 us (3%)
  other arithmetic  4.24 us (3%)
    psum x1, blocking collectives, on_device(): totals = lax.psum((counts, prob_sums, live_total), ('dp', 'expert'))  56.2 us
    all_to_all x1, blocking collectives, on_device(): lax.all_to_all(sent, 'expert', split_axis=0, concat_axis=0, tiled=True)  52 us
    dot_general x1, matrix products, expert_ffn(): jnp.einsum('skcd,kdf->skcf', tokens, w_in, preferred_element_type=jnp.flo...  18.7 us
    dot_general x1, matrix products, expert_ffn(): jnp.einsum('skcf,kfd->skcd', hidden, w_out, preferred_element_type=jnp.fl...  11.4 us
    ppermute x1, waiting for transfers between devices, shifted(): return lax.ppermute(block, axis, route)  5.31 us
    ppermute x1, starting transfers between devices, shifted(): return lax.ppermute(block, axis, route)  4.9 us
    all_to_all x1, starting transfers between devices, on_device(): lax.all_to_all(partial_value.reshape(devices, local_count * CAP, model_wi...  3.74 us
  transfers between devices with their start and end apart: 2, of which 1 were waited for; matrix products, arithmetic and copies ran while one was open for 4% of the time, Pallas kernels for 0%

commit v1 on v0

--- a/solution.py
+++ b/solution.py
@@ -1,7 +1,13 @@
+import functools
+
 import jax
 import jax.numpy as jnp
 from jax import lax
+from jax.experimental import pallas as pl
+from jax.experimental.pallas import tpu as pltpu
 from jax.sharding import PartitionSpec as P
+
+MESH = pl.DeviceIdType.MESH
 
 EXPERTS = 32
 TOP = 6
@@ -86,9 +92,493 @@
     return (result[None], balance.reshape(1))
 
 
+STAGES = ((0, 1, 2, 3),)
+WIDE = 512
+
+
+def nearest(me, pos, count):
+    found = 0
+    for own in range(count):
+        order = sorted(range(count), key=lambda other: (abs(other - own), other))
+        found = found + jnp.where(me == own, order[pos], 0)
+    return found
+
+
+def relay_kernel(
+    pipes, dps, line, live, rows,
+    route_ref, embedded_ref, section_ref, w_in_ref, w_out_ref,
+    mixed_ref, balance_ref,
+    win, wout, tokens, tail, info, slots_in, slots_out, own_part, to_mate, from_mate,
+    sent, from_left, from_right,
+    w_sem, shift_send, own_recv, tail_sem, right_send, left_send, mate_send, mate_recv,
+    info_send, info_recv, part_send, part_recv, back_send, left_recv, right_recv,
+):
+    p, d, y = lax.axis_index("pipe"), lax.axis_index("dp"), lax.axis_index("expert")
+    mate = 1 - d
+    tok_count, model_width = mixed_ref.shape
+    half_count = win.shape[0]
+    local_count = w_in_ref.shape[0]
+    hidden_width = wout.shape[1]
+    chunks = live // rows
+    groups = dps * line
+    experts = (line // 2) * local_count
+    per_expert = dps * CAP
+    slot_count = half_count * per_expert
+    f32 = jnp.float32
+    bf16 = jnp.bfloat16
+
+    def w_copies(k):
+        entry = d * half_count + k
+        return (
+            pltpu.make_async_copy(w_in_ref.at[entry], win.at[k], w_sem.at[0, k]),
+            pltpu.make_async_copy(w_out_ref.at[entry], wout.at[k], w_sem.at[1, k]),
+        )
+
+    barrier = pltpu.get_barrier_semaphore()
+    for g in range(1, groups):
+        other = lax.rem(d * line + y + g, groups)
+        pl.semaphore_signal(
+            barrier, inc=1, device_id=(p, other // line, lax.rem(other, line)), device_id_type=MESH
+        )
+
+    @pl.when(p > 0)
+    def _():
+        pl.semaphore_signal(barrier, inc=1, device_id=(p - 1, d, y), device_id_type=MESH)
+
+    @pl.when(p < pipes - 1)
+    def _():
+        pl.semaphore_signal(barrier, inc=1, device_id=(p + 1, d, y), device_id_type=MESH)
+
+    def own_rows(c):
+        return pl.ds(pl.multiple_of(d * tok_count + c * rows, rows), rows)
+
+    def mate_rows(c):
+        return pl.ds(pl.multiple_of(mate * tok_count + c * rows, rows), rows)
+
+    tail_rows = tok_count - live
+
+    def local_in(c):
+        return pltpu.make_async_copy(
+            embedded_ref.at[pl.ds(c * rows, rows)], tokens.at[y, own_rows(c)], own_recv.at[y, c]
+        )
+
+    local_tail = pltpu.make_async_copy(embedded_ref.at[pl.ds(live, tail_rows)], tail, tail_sem.at[1])
+
+    @pl.when(p == 0)
+    def _():
+        for c in range(chunks):
+            local_in(c).start()
+        local_tail.start()
+
+    ids = route_ref[0:8, :]
+    expert_of = lax.broadcasted_iota(jnp.int32, (experts, tok_count), 0).astype(f32)
+    hits = [(ids[k : k + 1, :] == expert_of).astype(f32) for k in range(TOP)]
+    total = hits[0]
+    for k in range(1, TOP):
+        total = total + hits[k]
+    before = (
+        lax.broadcasted_iota(jnp.int32, (tok_count, tok_count), 0)
+        < lax.broadcasted_iota(jnp.int32, (tok_count, tok_count), 1)
+    ).astype(f32).astype(bf16)
+    earlier = jnp.dot(total.astype(bf16), before, preferred_element_type=f32)
+    me = d * line + y
+    info[me, 0:8, :] = jnp.full((8, tok_count), -1.0, f32)
+    for k in range(TOP):
+        rank = jnp.sum(hits[k] * earlier, axis=0, keepdims=True)
+        id_k = ids[k : k + 1, :]
+        keep = (id_k >= 0.0) & (rank < CAP)
+        code = id_k * per_expert + (d * CAP).astype(f32) + rank
+        info[me, k : k + 1, :] = jnp.where(keep, code, -1.0)
+    info[me, 8:24, :] = jnp.concatenate([route_ref[8:16, :], ids], axis=0)
+
+    for z in range(line):
+        for e in range(dps):
+            lo = e * tok_count + live
+            tokens[z, lo : lo + tail_rows, :] = jnp.zeros((tail_rows, model_width), bf16)
+
+    pl.semaphore_wait(barrier, groups - 1 + (p > 0).astype(jnp.int32) + (p < pipes - 1).astype(jnp.int32))
+
+    def shift(c):
+        return pltpu.make_async_remote_copy(
+            src_ref=section_ref.at[pl.ds(c * rows, rows)],
+            dst_ref=tokens.at[y, own_rows(c)],
+            send_sem=shift_send.at[c],
+            recv_sem=own_recv.at[y, c],
+            device_id=(p + 1, d, y),
+            device_id_type=MESH,
+        )
+
+    shift_tail = pltpu.make_async_remote_copy(
+        src_ref=section_ref.at[pl.ds(live, tail_rows)],
+        dst_ref=tail,
+        send_sem=tail_sem.at[0],
+        recv_sem=tail_sem.at[1],
+        device_id=(p + 1, d, y),
+        device_id_type=MESH,
+    )
+
+    @pl.when(p < pipes - 1)
+    def _():
+        for c in range(chunks):
+            shift(c).start()
+        shift_tail.start()
+
+    def info_copy(g):
+        other = lax.rem(me + g, groups)
+        return pltpu.make_async_remote_copy(
+            src_ref=info.at[me],
+            dst_ref=info.at[me],
+            send_sem=info_send.at[g],
+            recv_sem=info_recv.at[me],
+            device_id=(p, other // line, lax.rem(other, line)),
+            device_id_type=MESH,
+        )
+
+    for g in range(1, groups):
+        info_copy(g).start()
+
+    @pl.loop(0, half_count)
+    def _(k):
+        for copy in w_copies(k):
+            copy.start()
+
+    def along(z, c, send_sem, target):
+        return pltpu.make_async_remote_copy(
+            src_ref=tokens.at[z, own_rows(c)],
+            dst_ref=tokens.at[z, own_rows(c)],
+            send_sem=send_sem.at[z, c],
+            recv_sem=own_recv.at[z, c],
+            device_id=(p, d, target),
+            device_id_type=MESH,
+        )
+
+    def across(z, c):
+        return pltpu.make_async_remote_copy(
+            src_ref=tokens.at[z, own_rows(c)],
+            dst_ref=tokens.at[z, own_rows(c)],
+            send_sem=mate_send.at[z, c],
+            recv_sem=mate_recv.at[z, c],
+            device_id=(p, mate, y),
+            device_id_type=MESH,
+        )
+
+    def codes_of(e, z):
+        return info[e * line + z]
+
+    base = ((y // 2) * local_count + d * half_count) * per_expert
+
+    def dispatch(pos):
+        z = nearest(y, pos, line)
+        code = jnp.concatenate([codes_of(e, z)[0:8, :] for e in range(dps)], axis=1) - base.astype(f32)
+        slot_of = lax.broadcasted_iota(jnp.int32, (slot_count, dps * tok_count), 0).astype(f32)
+        taken = (code[0:1, :] == slot_of).astype(f32)
+        for k in range(1, TOP):
+            taken = taken + (code[k : k + 1, :] == slot_of).astype(f32)
+        taken = taken.astype(bf16)
+
+        @pl.loop(0, model_width // WIDE)
+        def _(n):
+            cols = pl.ds(pl.multiple_of(n * WIDE, WIDE), WIDE)
+            picked = jnp.dot(taken, tokens[z, :, cols], preferred_element_type=f32).astype(bf16)
+            slots_in[pos, :, :, cols] = picked.reshape(half_count, per_expert, WIDE)
+
+    def forward(pos, c):
+        z = nearest(y, pos, line)
+        pltpu.make_async_copy(tokens.at[z, own_rows(c)], tokens.at[z, own_rows(c)], own_recv.at[z, c]).wait()
+
+        @pl.when((z <= y) & (y < line - 1))
+        def _():
+            along(z, c, right_send, y + 1).start()
+
+        @pl.when((z >= y) & (y > 0))
+        def _():
+            along(z, c, left_send, y - 1).start()
+
+        across(z, c).start()
+
+    def mate_arrived(pos):
+        z = nearest(y, pos, line)
+        for c in range(chunks):
+            pltpu.make_async_copy(
+                tokens.at[z, mate_rows(c)], tokens.at[z, mate_rows(c)], mate_recv.at[z, c]
+            ).wait()
+
+    for pos in range(line):
+        for c in range(chunks):
+            forward(pos, c)
+        if pos == 0:
+            for g in range(1, groups):
+                other = lax.rem(me + g, groups)
+                pltpu.make_async_copy(info.at[other], info.at[other], info_recv.at[other]).wait()
+        else:
+            mate_arrived(pos - 1)
+            dispatch(pos - 1)
+    mate_arrived(line - 1)
+    dispatch(line - 1)
+
+    def against(x, columns):
+        return lax.dot_general(x, columns, (((1,), (1,)), ((), ())), preferred_element_type=f32)
+
+    for index, stage in enumerate(STAGES):
+        first, last = stage[0], stage[-1] + 1
+        count = (last - first) * per_expert
+
+        @pl.loop(0, half_count)
+        def _(k):
+            if index == 0:
+                for copy in w_copies(k):
+                    copy.wait()
+            x = slots_in[first:last, k].reshape(count, model_width)
+            gate = against(x, win[k, :hidden_width])
+            up = against(x, win[k, hidden_width:])
+            hidden = (gate * (1.0 / (1.0 + jnp.exp(-gate))) * up).astype(bf16)
+
+            @pl.loop(0, model_width // WIDE)
+            def _(n):
+                cols = pl.ds(pl.multiple_of(n * WIDE, WIDE), WIDE)
+                out = jnp.dot(hidden, wout[k, :, cols], preferred_element_type=f32).astype(bf16)
+                slots_out[first:last, k, :, cols] = out.reshape(last - first, per_expert, WIDE)
+
+    def mix(pos, e, store):
+        z = nearest(y, pos, line)
+        record = info[e * line + z]
+        code = record[0:8, :] - base.astype(f32)
+        slot_of = lax.broadcasted_iota(jnp.int32, (slot_count, tok_count), 0).astype(f32)
+        weights = jnp.zeros((slot_count, tok_count), f32)
+        for k in range(TOP):
+            weights = weights + jnp.where(code[k : k + 1, :] == slot_of, record[8 + k : 9 + k, :], 0.0)
+        weights = weights.T
+        high = weights.astype(bf16)
+        low = (weights - high.astype(f32)).astype(bf16)
+
+        @pl.loop(0, model_width // WIDE)
+        def _(n):
+            cols = pl.ds(pl.multiple_of(n * WIDE, WIDE), WIDE)
+            values = slots_out[pos, :, :, cols].reshape(slot_count, WIDE)
+            part = jnp.dot(high, values, preferred_element_type=f32) + jnp.dot(
+                low, values, preferred_element_type=f32
+            )
+            store(cols, part[:live])
+
+    def part_copy(pos):
+        z = nearest(y, pos, line)
+        return pltpu.make_async_remote_copy(
+            src_ref=to_mate.at[z],
+            dst_ref=from_mate.at[z],
+            send_sem=part_send.at[z],
+            recv_sem=part_recv.at[z],
+            device_id=(p, mate, y),
+            device_id_type=MESH,
+        )
+
+    def partials(pos):
+        z = nearest(y, pos, line)
+
+        def store_mate(cols, part):
+            to_mate[z, :, cols] = part.astype(bf16)
+
+        def store_own(cols, part):
+            own_part[z, :, cols] = part
+
+        mix(pos, mate, store_mate)
+        part_copy(pos).start()
+        mix(pos, d, store_own)
+
+    def back(z, c, buffer, recv_sem, target):
+        span = pl.ds(c * rows, rows)
+        return pltpu.make_async_remote_copy(
+            src_ref=sent.at[z, span],
+            dst_ref=buffer.at[z, span],
+            send_sem=back_send.at[z, c],
+            recv_sem=recv_sem.at[z, c],
+            device_id=(p, d, target),
+            device_id_type=MESH,
+        )
+
+    def arrived(buffer, z, c, recv_sem):
+        span = pl.ds(c * rows, rows)
+        pltpu.make_async_copy(buffer.at[z, span], buffer.at[z, span], recv_sem.at[z, c]).wait()
+
+    def pass_on(z, c, upstream, buffer, recv_sem, target):
+        span = pl.ds(c * rows, rows)
+
+        @pl.when(upstream)
+        def _():
+            arrived(buffer, z, c, recv_sem)
+            sent[z, span] = (
+                own_part[z, span] + from_mate[z, span].astype(f32) + buffer[z, span].astype(f32)
+            ).astype(bf16)
+
+        @pl.when(jnp.logical_not(upstream))
+        def _():
+            sent[z, span] = (own_part[z, span] + from_mate[z, span].astype(f32)).astype(bf16)
+
+        back(z, c, buffer, recv_sem, target).start()
+
+    def chain(pos):
+        z = nearest(y, pos, line)
+        part_copy(pos).wait_recv()
+
+        @pl.when(z > y)
+        def _():
+            for c in range(chunks):
+                pass_on(z, c, y > 0, from_left, left_recv, y + 1)
+
+        @pl.when(z < y)
+        def _():
+            for c in range(chunks):
+                pass_on(z, c, y < line - 1, from_right, right_recv, y - 1)
+
+    for pos in range(line - 1, -1, -1):
+        partials(pos)
+        if pos < line - 1:
+            chain(pos + 1)
+
+    counts = jnp.zeros((experts, tok_count), f32)
+    probs = jnp.zeros((experts, tok_count), f32)
+    real = jnp.zeros((1, tok_count), f32)
+    for g in range(groups):
+        record = info[g]
+        for k in range(TOP):
+            hit = record[16 + k : 17 + k, :] == expert_of
+            counts = counts + hit.astype(f32)
+            probs = probs + jnp.where(hit, record[8 + k : 9 + k, :], 0.0)
+        real = real + (record[16:17, :] >= 0.0).astype(f32)
+    by_expert = jnp.sum(counts, axis=1, keepdims=True) * jnp.sum(probs, axis=1, keepdims=True)
+    live_total = jnp.sum(real, axis=1, keepdims=True)
+    balance = experts * jnp.sum(by_expert, axis=0, keepdims=True) / (TOP * live_total * live_total)
+    balance_ref[...] = jnp.broadcast_to(balance, balance_ref.shape)
+
+    part_copy(0).wait_recv()
+
+    @pl.when(p < pipes - 1)
+    def _():
+        shift_tail.wait_send()
+
+    pltpu.make_async_copy(tail, tail, tail_sem.at[1]).wait()
+    mixed_ref[live:, :] = tail[...]
+    for c in range(chunks):
+        span = pl.ds(c * rows, rows)
+        own_part[y, span] = (
+            own_part[y, span]
+            + from_mate[y, span].astype(f32)
+            + tokens[y, own_rows(c), :].astype(f32)
+        )
+
+        @pl.when(y > 0)
+        def _():
+            arrived(from_left, y, c, left_recv)
+            own_part[y, span] = own_part[y, span] + from_left[y, span].astype(f32)
+
+        @pl.when(y < line - 1)
+        def _():
+            arrived(from_right, y, c, right_recv)
+            own_part[y, span] = own_part[y, span] + from_right[y, span].astype(f32)
+
+        mixed_ref[span, :] = own_part[y, span].astype(bf16)
+
+    for g in range(1, groups):
+        info_copy(g).wait_send()
+
+    @pl.when(p < pipes - 1)
+    def _():
+        for c in range(chunks):
+            shift(c).wait_send()
+
+    for pos in range(line):
+        z = nearest(y, pos, line)
+        part_copy(pos).wait_send()
+        for c in range(chunks):
+            across(z, c).wait_send()
+
+            @pl.when((z <= y) & (y < line - 1))
+            def _():
+                along(z, c, right_send, y + 1).wait_send()
+
+            @pl.when((z >= y) & (y > 0))
+            def _():
+                along(z, c, left_send, y - 1).wait_send()
+
+            if pos > 0:
+                back(z, c, from_left, left_recv, y).wait_send()
+
+
+def fused(sizes, embedded, section_out, expert_ids, route_weights, valid_tokens, w_gate_up, w_down):
+    pipes, dps, line = sizes["pipe"], sizes["dp"], sizes["expert"]
+    tok_count, model_width = embedded.shape
+    local_count, _, both_width = w_gate_up.shape[1:]
+    hidden_width = w_down.shape[2]
+    half_count = local_count // dps
+    live = tok_count * 3 // 4
+    rows = 32
+    chunks = live // rows
+    groups = dps * line
+    per_expert = dps * CAP
+    live_row = jnp.arange(tok_count, dtype=jnp.int32)[None, :] < valid_tokens[0, 0]
+    ids = jnp.where(live_row, expert_ids[0].T, -1).astype(jnp.float32)
+    pad = ((0, 8 - TOP), (0, 0))
+    route_in = jnp.concatenate(
+        [jnp.pad(ids, pad, constant_values=-1.0), jnp.pad(route_weights[0].T, pad)], axis=0
+    )
+    bf16, f32 = jnp.bfloat16, jnp.float32
+    dma = pltpu.SemaphoreType.DMA
+    vmem = pl.BlockSpec(memory_space=pltpu.VMEM)
+    hbm = pl.BlockSpec(memory_space=pl.ANY)
+    mixed, balance = pl.pallas_call(
+        functools.partial(relay_kernel, pipes, dps, line, live, rows),
+        out_shape=(
+            jax.ShapeDtypeStruct((tok_count, model_width), bf16),
+            jax.ShapeDtypeStruct((8, 128), f32),
+        ),
+        in_specs=[vmem, hbm, hbm, hbm, hbm],
+        out_specs=(vmem, vmem),
+        scratch_shapes=[
+            pltpu.VMEM((half_count, both_width, model_width), bf16),
+            pltpu.VMEM((half_count, hidden_width, model_width), bf16),
+            pltpu.VMEM((line, dps * tok_count, model_width), bf16),
+            pltpu.VMEM((tok_count - live, model_width), bf16),
+            pltpu.VMEM((groups, 24, tok_count), f32),
+            pltpu.VMEM((line, half_count, per_expert, model_width), bf16),
+            pltpu.VMEM((line, half_count, per_expert, model_width), bf16),
+            pltpu.VMEM((line, live, model_width), f32),
+            pltpu.VMEM((line, live, model_width), bf16),
+            pltpu.VMEM((line, live, model_width), bf16),
+            pltpu.VMEM((line, live, model_width), bf16),
+            pltpu.VMEM((line, live, model_width), bf16),
+            pltpu.VMEM((line, live, model_width), bf16),
+            dma((2, half_count)),
+            dma((chunks,)),
+            dma((line, chunks)),
+            dma((2,)),
+            dma((line, chunks)),
+            dma((line, chunks)),
+            dma((line, chunks)),
+            dma((line, chunks)),
+            dma((groups,)),
+            dma((groups,)),
+            dma((line,)),
+            dma((line,)),
+            dma((line, chunks)),
+            dma((line, chunks)),
+            dma((line, chunks)),
+        ],
+        compiler_params=pltpu.CompilerParams(
+            collective_id=0, has_side_effects=True, vmem_limit_bytes=67043328
+        ),
+    )(route_in, embedded, section_out[0], jnp.swapaxes(w_gate_up[0], 1, 2), w_down[0])
+    return mixed[None], balance[0, :1]
+
+
+def step(sizes, *args):
+    local_count = args[5].shape[1]
+    if sizes["dp"] == 2 and sizes["expert"] == 4 and local_count % 2 == 0:
+        return fused(sizes, *args)
+    return on_device(*args)
+
+
 def solution(mesh):
     return jax.shard_map(
-        on_device,
+        functools.partial(step, dict(mesh.shape)),
         mesh=mesh,
         in_specs=(
             P(("dp", "expert"), None),

time: 169 us -> 97.9 us (0.58)
  blocking collectives: 108 us -> 0 us
  Pallas kernels: 0 us -> 90 us
  matrix products: 33 us -> 0 us
  starting transfers between devices: 8.64 us -> 0 us
  waiting for transfers between devices: 5.32 us -> 0 us
  between operations: 4.57 us -> 1.29 us
  other arithmetic: 4.24 us -> 1.3 us
    pallas_call x0 -> x1, Pallas kernels: none -> 90 us  [fused(): pl.pallas_call(functools.partial(relay_kernel, pipes, dps, line, live, ro...]
    psum x1 -> x0, blocking collectives: 56.2 us -> none  [on_device(): totals = lax.psum((counts, prob_sums, live_total), ('dp', 'expert'))]
    all_to_all x1 -> x0, blocking collectives: 52 us -> none  [on_device(): lax.all_to_all(sent, 'expert', split_axis=0, concat_axis=0, tiled=True)]
    dot_general x4 -> x0, matrix products: 33 us -> none  [the longest x1 18.7 us: expert_ffn(): jnp.einsum('skcd,kdf->skcf', tokens, w_in, preferred_element_type=jnp.flo...]
    ppermute x1 -> x0, waiting for transfers between devices: 5.31 us -> none  [shifted(): return lax.ppermute(block, axis, route)]
    ppermute x1 -> x0, starting transfers between devices: 4.9 us -> none  [shifted(): return lax.ppermute(block, axis, route)]
    all_to_all x1 -> x0, starting transfers between devices: 3.74 us -> none  [on_device(): lax.all_to_all(partial_value.reshape(devices, local_count * CAP, model_wi...]
    another operation x2 -> x0, other arithmetic: 1.77 us -> none
  transfers between devices with their start and end apart: 2 -> 0, of which waited for: 1 -> 0; matrix products, arithmetic and copies ran while one was open for 4% -> 0% of each run, Pallas kernels for 0% -> 0%
where the time goes in v1:
time: 97.9 us; the launch traced here: 96.3 us
  Pallas kernels  90 us (92%)
  local copies, waits for them, and re-layouts  3.75 us (4%)
  other arithmetic  1.3 us (1%)
  between operations  1.29 us (1%)
    pallas_call x1, Pallas kernels, fused(): pl.pallas_call(functools.partial(relay_kernel, pipes, dps, line, live, ro...  90 us
    unnamed x2, local copies, waits for them, and re-layouts  2.56 us

profile of v1, /device:TPU:0, one launch (start us, length us, event | category | flops | bytes accessed | tf_op | source)
XLA Modules:
  0.0 96.3 jit_solution(18313668723565216394)
XLA Ops:
  1.3 0.7 fusion.1
  2.0 0.7 copy.13
  2.7 0.6 select_maximum_fusion.route_ref
  3.3 90.0 %shard_map.86 = (bf16[128,2048]{1,0:T(8,128)(2,1)}, f32[8,128]{1,0:T(8,128)}) custom-call(f32[16,128]{1,0:T(8,128)} %select_maximum_fusion.route_ref, bf16[128,2048]{1,0:T(8,128)(2,1)} %embedded_ref.1, bf16[128,2048]{1,0:T(8,128)(2,1)} %bitcast.24, bf16[16,704,2048]{2,1,0:T(8,128)(2,1)} %bitcast.22, bf16[16,352,2048]{2,1,0:T(8,128)(2,1)} %bitcast.23), custom_call_target="tpu_custom_call" | custom-call | tf_op jit(solution)/shard_map/pallas_call | solution.py:527
  93.3 1.2 %slice.3 = f32[1,1]{1,0:T(1,128)} slice(f32[8,128]{1,0:T(8,128)} %get-tuple-element.5), slice={[0:1], [0:1]} | slice | bytes 8 | tf_op jit(solution)/shard_map/slice | solution.py:569
  94.5 1.9 %copy.16 = bf16[1,128,2048]{2,1,0:T(8,128)(2,1)} copy(bf16[1,128,2048]{2,1,0:T(8,128)(2,1)} %bitcast.25) | data formatting | bytes 1048576
  (1 shorter events, 0.0 us)
